TPU v7x, 32 devices: a whole 2x2x4 slice. The times are simulated.
32 devices in a mesh: member: 2 (over y), pts: 4 (over x, core), sub: 4 (over z).
Axes of the slice: x: 2, y: 2, z: 4, core: 2. Of those that a mesh axis runs over, the one named last changes fastest.
Arguments:
- spectrum: bfloat16 [1800, 32, 512], P(None, ('member', 'pts'), 'sub'), parts along dimension 1, may hold values from 0.049804688 to 2
- interaction: bfloat16 [1800, 1800], replicated, may hold values from -0.125 to 0.125
- speeds: float32 [1800], replicated, may hold values from 0.2 to 0.7
- mask: int32 [16, 512], P('pts', 'sub'), may hold values from 0 to 1, as said below
Outputs:
- evolved: bfloat16 [1800, 32, 512], P(None, ('member', 'pts'), 'sub'), parts along dimension 1
There are 2 independent parts, one for each index of `member`. A program takes and returns all parts, laid end to end along the dimension named above; an argument that names none is the same for every part. Nothing has to cross between parts.
Inputs may be any that keep to these rules, and one draw needn't show every extreme that they name: `mask`: 1 marks sea, 0 land; the share of sea differs from grid row to grid row.
All inputs are finite; a program needn't handle non-finite values.
Results may differ from a plain program's by a relative error of at most 0.0075.
Values may be sent and summed in bfloat16 or wider, within the bound.
A program may use at most 128 MiB of HBM per device.

v0:
```python
import functools
import math

import jax
import jax.numpy as jnp
import numpy as np
from jax import lax
from jax.experimental import pallas as pl
from jax.experimental.pallas import tpu as pltpu
from jax.sharding import PartitionSpec as P

ND = 36
PROP = 2
UNIT = 72
SUB = 8
CHUNKS = 4
SLOTS = 1

coupling = 0.5


def circle():
    angle = np.arange(ND, dtype=np.int32).astype(np.float32) * np.float32(2.0 * math.pi / ND)
    angle = angle.astype(np.float64)
    return np.cos(angle).astype(np.float32), np.sin(angle).astype(np.float32)


def runs(flags):
    found, start = [], None
    for i, flag in enumerate(list(flags) + [False]):
        if flag and start is None:
            start = i
        if not flag and start is not None:
            found.append((start, i - start))
            start = None
    return found


def tables(lanes):
    cosine, sine = circle()
    d = np.arange(UNIT) % ND
    rows = [np.abs(cosine[d]), np.abs(sine[d]), cosine[d] > 0, sine[d] > 0]
    return np.stack([np.broadcast_to(r.astype(np.float32)[:, None], (UNIT, lanes)) for r in rows])


def splits(blocks):
    size = max(2, blocks // CHUNKS // 2 * 2)
    starts = list(range(0, blocks, size))
    if len(starts) > 1 and blocks - starts[-1] < size:
        starts.pop()
    return [(s, (starts[i + 1] if i + 1 < len(starts) else blocks) - s) for i, s in enumerate(starts)]


def kernel(
    rows_x, chunks, plus_runs, minus_runs, counts,
    spec_hbm, inter_hbm, speeds_ref, mask_ref, tabs_ref, outv,
    specv, inter, flat, acc, field, first, column, stage, outs, packed, arrived, halo,
    xsend, xrecv, ysend, yrecv,
    load_sem, send_sem, recv_sem,
):
    lanes = flat.shape[1] // rows_x
    blocks = field.shape[1]
    tile_count = UNIT // SUB
    px, sy = lax.axis_index("pts"), lax.axis_index("sub")
    nx, ny = counts
    partner = [{"pts": px + 1}, {"pts": px - 1}, {"sub": sy + 1}, {"sub": sy - 1}]
    sends = [px < nx - 1, px > 0, sy < ny - 1, sy > 0]
    receives = [sends[1], sends[0], sends[3], sends[2]]

    spec_copy = pltpu.make_async_copy(spec_hbm, specv, load_sem.at[len(chunks)])
    spec_copy.start()
    inter_copies = []
    for c, (start, count) in enumerate(chunks):
        part = pl.ds(start * UNIT, count * UNIT)
        copy = pltpu.make_async_copy(inter_hbm.at[part], inter.at[part], load_sem.at[c])
        copy.start()
        inter_copies.append(copy)

    barrier = pltpu.get_barrier_semaphore()
    for kind in range(4):
        @pl.when(sends[kind])
        def _():
            pl.semaphore_signal(
                barrier, inc=1, device_id=partner[kind], device_id_type=pl.DeviceIdType.MESH
            )

    def exchange(e, c, kind):
        start, count = chunks[c]
        part = pl.ds(start, count)
        if kind < 2:
            source, target = xsend.at[e, kind, part], xrecv.at[e, kind, part]
        else:
            source, target = ysend.at[e, part], yrecv.at[e, kind - 2, part]
        return pltpu.make_async_remote_copy(
            src_ref=source, dst_ref=target,
            send_sem=send_sem.at[e, c, kind], recv_sem=recv_sem.at[e, c, kind],
            device_id=partner[kind], device_id_type=pl.DeviceIdType.MESH,
        )

    def start_sends(e, c):
        for kind in range(4):
            @pl.when(sends[kind])
            def _():
                exchange(e, c, kind).start()

    def wait_receives(e, c):
        for kind in range(4):
            @pl.when(receives[kind])
            def _():
                exchange(e, c, kind).wait_recv()

    for kind in range(4):
        @pl.when(jnp.logical_not(receives[kind]))
        def _():
            for e in range(PROP):
                if kind < 2:
                    xrecv[e, kind] = jnp.zeros(xrecv.shape[2:], xrecv.dtype)
                else:
                    yrecv[e, kind - 2] = jnp.zeros(yrecv.shape[2:], yrecv.dtype)

    comps = flat.shape[0]
    starts = list(range(0, comps - lanes + 1, lanes))
    if comps % lanes:
        starts.append(comps - lanes)
    for at in starts:
        row = jnp.broadcast_to(speeds_ref[0:1, at : at + lanes], (lanes, lanes))
        column[at : at + lanes, :] = row.T

    spec_copy.wait()

    def spread(block, count):
        length = count * UNIT
        whole = specv[pl.ds(pl.multiple_of(block * (rows_x * UNIT), 16), rows_x * length), :]
        stage[0 : rows_x * length, :] = whole.astype(jnp.float32)
        for x in range(rows_x):
            values = stage[pl.ds(x, length, stride=rows_x), :]
            flat[pl.ds(pl.multiple_of(block * UNIT, 16), length), x * lanes : (x + 1) * lanes] = (
                values.astype(jnp.bfloat16)
            )
            for b in range(count):
                field[x, block + b] = values[b * UNIT : (b + 1) * UNIT]

    @pl.loop(0, blocks // 2)
    def _(i):
        spread(2 * i, 2)

    if blocks % 2:
        spread(blocks - 1, 1)

    pl.semaphore_wait(barrier, sum(s.astype(jnp.int32) for s in sends))

    lane = lax.broadcasted_iota(jnp.int32, (SUB, lanes), 1)
    pair = lane // 2
    even = lane % 2 == 0
    sea = [
        jnp.broadcast_to(mask_ref[x : x + 1, :].astype(jnp.float32), (SUB, lanes))
        for x in range(rows_x)
    ]
    cosine, sine = (np.resize(v, UNIT).reshape(tile_count, SUB) for v in circle())

    def sides(t):
        found = []
        for values in (cosine[t], sine[t]):
            if np.all(values >= 0):
                found.append(True)
            elif np.all(values <= 0):
                found.append(False)
            else:
                found.append(None)
        return found

    def pack_x(e, block, slot, source):
        for kind, group, x in ((0, plus_runs, rows_x - 1), (1, minus_runs, 0)):
            at = 0
            for begin, length in group:
                packed[slot, kind, at : at + length, :] = source[x, block, begin : begin + length, :]
                at += length
            xsend[e, kind, block] = packed[slot, kind].astype(xsend.dtype)

    def grow_block(base, i, slot):
        block = base + i
        message = jnp.zeros((SUB, lanes), jnp.float32)
        for t in range(tile_count):
            part = slice(t * SUB, (t + 1) * SUB)
            place = pl.ds(pl.multiple_of(i * UNIT, SUB) + t * SUB, SUB)
            for x in range(rows_x):
                wide = field[x, block, part, :]
                coupled = acc[place, x * lanes : (x + 1) * lanes]
                grown = (wide + coupling * wide * coupled) * sea[x]
                grown = grown.astype(jnp.bfloat16).astype(jnp.float32)
                field[x, block, part, :] = grown
                j = t * rows_x + x
                message = jnp.where(pair == j, pltpu.roll(grown, 2 * j + 1, 1), message)
        ysend[0, block] = message
        pack_x(0, block, slot, field)

    def halos(e, block, slot):
        for kind, group in ((0, plus_runs), (1, minus_runs)):
            arrived[slot, kind] = xrecv[e, kind, block].astype(jnp.float32)
            at = 0
            for begin, length in group:
                halo[slot, begin : begin + length, :] = arrived[slot, kind, at : at + length, :]
                at += length

    def advance_block(e, block, slot):
        source = field if e == 0 else first
        results = []
        edges = jnp.where(even, pltpu.roll(yrecv[e, 0, block], 2, 1), yrecv[e, 1, block])
        message = jnp.zeros((SUB, lanes), jnp.float32)
        for t in range(tile_count):
            part = slice(t * SUB, (t + 1) * SUB)
            speed = column[pl.ds(pl.multiple_of(block * UNIT, SUB) + t * SUB, SUB), :]
            cross, along = speed * tabs_ref[0, part, :], speed * tabs_ref[1, part, :]
            side_x, side_y = sides(t)
            up_x = tabs_ref[2, part, :] > 0.5 if side_x is None else None
            if side_y is None:
                up_y = tabs_ref[3, part, :] > 0.5
                edge = jnp.where(up_y, lane, lanes - 1 - lane) == 0
            else:
                edge = lane == (0 if side_y else lanes - 1)
            tiles = [source[x, block, part, :] for x in range(rows_x)]
            outer = halo[slot, part, :]
            for x in range(rows_x):
                j = t * rows_x + x
                here = tiles[x]
                lower = tiles[x - 1] if x > 0 else outer
                higher = tiles[x + 1] if x < rows_x - 1 else outer
                if side_x is None:
                    near_x = jnp.where(up_x, lower, higher)
                else:
                    near_x = lower if side_x else higher
                if side_y is None:
                    near_y = jnp.where(up_y, pltpu.roll(here, 1, 1), pltpu.roll(here, lanes - 1, 1))
                else:
                    near_y = pltpu.roll(here, 1 if side_y else lanes - 1, 1)
                near_y = jnp.where(edge, pltpu.roll(edges, lanes - (2 * j + 2), 1), near_y)
                result = (here - cross * (here - near_x) - along * (here - near_y)) * sea[x]
                results.append(result)
                if e == 0:
                    message = jnp.where(pair == j, pltpu.roll(result, 2 * j + 1, 1), message)
        for t in range(tile_count):
            for x in range(rows_x):
                result = results[t * rows_x + x]
                if e == 0:
                    first[x, block, t * SUB : (t + 1) * SUB, :] = result
                else:
                    outs[slot, pl.ds(x + t * SUB * rows_x, SUB, stride=rows_x), :] = result
        if e == 0:
            ysend[1, block] = message
            pack_x(1, block, slot, first)
        else:
            size = rows_x * UNIT
            outv[pl.ds(pl.multiple_of(block * size, 16), size), :] = outs[slot].astype(outv.dtype)

    def several(count, body):
        @pl.loop(0, count // SLOTS)
        def _(i):
            body([i * SLOTS + u for u in range(SLOTS)])

        if count % SLOTS:
            body([count - count % SLOTS + u for u in range(count % SLOTS)])

    def multiply(c):
        start, count = chunks[c]
        inter_copies[c].wait()
        acc[0 : count * UNIT, :] = jnp.dot(
            inter[start * UNIT : (start + count) * UNIT, :], flat[...],
            preferred_element_type=jnp.float32,
        )

        def body(which):
            for slot, i in enumerate(which):
                grow_block(start, i, slot)

        several(count, body)
        start_sends(0, c)

    def advance(e, c):
        start, count = chunks[c]
        wait_receives(e, c)

        def body(which):
            for slot, i in enumerate(which):
                halos(e, start + i, slot)
            for slot, i in enumerate(which):
                advance_block(e, start + i, slot)

        several(count, body)
        if e == 0:
            start_sends(1, c)

    total = len(chunks)
    for c in range(total):
        multiply(c)
        if c >= 2:
            advance(0, c - 2)
    if total >= 2:
        advance(0, total - 2)
    for c in range(total - 3):
        advance(1, c)
    advance(0, total - 1)
    for c in range(max(total - 3, 0), total):
        advance(1, c)

    for e in range(PROP):
        for c in range(len(chunks)):
            for kind in range(4):
                @pl.when(sends[kind])
                def _():
                    exchange(e, c, kind).wait_send()


def flush(held, out_hbm, sem):
    copy = pltpu.make_async_copy(held, out_hbm, sem)
    copy.start()
    copy.wait()


def shards(mesh_counts, spectrum, interaction, speeds, mask):
    comps, rows_x, lanes = spectrum.shape
    blocks = comps // UNIT
    chunks = splits(blocks)
    most = max(count for _, count in chunks)
    cosine, sine = circle()
    plus = cosine[np.arange(UNIT) % ND] > 0
    plus_runs, minus_runs = runs(plus), runs(~plus)
    half = max(int(plus.sum()), int((~plus).sum()))
    any_space = pl.BlockSpec(memory_space=pltpu.HBM)
    vmem = pl.BlockSpec(memory_space=pltpu.VMEM)
    f32, bf16 = jnp.float32, jnp.bfloat16
    out = pl.pallas_call(
        functools.partial(kernel, rows_x, chunks, plus_runs, minus_runs, mesh_counts),
        out_shape=jax.ShapeDtypeStruct((comps * rows_x, lanes), bf16),
        in_specs=[any_space, any_space, vmem, vmem, vmem],
        out_specs=vmem,
        scratch_shapes=[
            pltpu.VMEM((comps * rows_x, lanes), bf16),
            pltpu.VMEM((comps, comps), bf16),
            pltpu.VMEM((comps, rows_x * lanes), bf16),
            pltpu.VMEM((most * UNIT, rows_x * lanes), f32),
            pltpu.VMEM((rows_x, blocks, UNIT, lanes), f32),
            pltpu.VMEM((rows_x, blocks, UNIT, lanes), f32),
            pltpu.VMEM((comps, lanes), f32),
            pltpu.VMEM((2 * UNIT * rows_x, lanes), f32),
            pltpu.VMEM((SLOTS, UNIT * rows_x, lanes), f32),
            pltpu.VMEM((SLOTS, 2, half, lanes), f32),
            pltpu.VMEM((SLOTS, 2, half, lanes), f32),
            pltpu.VMEM((SLOTS, UNIT, lanes), f32),
            pltpu.VMEM((PROP, 2, blocks, half, lanes), bf16),
            pltpu.VMEM((PROP, 2, blocks, half, lanes), bf16),
            pltpu.VMEM((PROP, blocks, SUB, lanes), f32),
            pltpu.VMEM((PROP, 2, blocks, SUB, lanes), f32),
            pltpu.SemaphoreType.DMA((len(chunks) + 1,)),
            pltpu.SemaphoreType.DMA((PROP, len(chunks), 4)),
            pltpu.SemaphoreType.DMA((PROP, len(chunks), 4)),
        ],
        compiler_params=pltpu.CompilerParams(
            collective_id=0, has_side_effects=True, vmem_limit_bytes=62 * 1024 * 1024
        ),
    )(
        spectrum.reshape(comps * rows_x, lanes), interaction, speeds.reshape(1, comps), mask,
        jnp.asarray(tables(lanes)),
    )
    out = pl.pallas_call(
        flush,
        out_shape=jax.ShapeDtypeStruct((comps * rows_x, lanes), bf16),
        in_specs=[vmem],
        out_specs=any_space,
        scratch_shapes=[pltpu.SemaphoreType.DMA],
        compiler_params=pltpu.CompilerParams(vmem_limit_bytes=8 * 1024 * 1024),
    )(out)
    return out.reshape(comps, rows_x, lanes)


def solution(mesh):
    placed = (P(None, ("member", "pts"), "sub"), P(), P(), P("pts", "sub"))
    return jax.shard_map(
        functools.partial(shards, (mesh.shape["pts"], mesh.shape["sub"])),
        mesh=mesh,
        in_specs=placed,
        out_specs=P(None, ("member", "pts"), "sub"),
        check_vma=False,
    )
```

profile of v0, /device:TPU:0, one launch (start us, length us, event | category | flops | bytes accessed | tf_op | source)
XLA Modules:
  0.0 31.9 jit_solution(15805673875410902577)
XLA Ops:
  0.0 1.3 %reshape.10.speeds_ref = f32[1,1800]{1,0:T(1,128)} reshape(f32[1800]{0:T(1024)} %param.7) | data formatting | bytes 14400 | tf_op jit(solution)/shard_map/reshape | solution.py:361
  1.3 27.9 %shard_map.55.held = bf16[7200,128]{1,0:T(8,128)(2,1)} custom-call(bf16[7200,128]{1,0:T(8,128)(2,1)} %bitcast.2, bf16[1800,1800]{1,0:T(8,128)(2,1)} %inter_hbm.1, f32[1,1800]{1,0:T(1,128)} %reshape.10.speeds_ref, s32[4,128]{1,0:T(4,128)} %mask_ref.1, f32[4,72,128]{2,1,0:T(8,128)} %constant.2.clone.tabs_ref), custom_call_target="tpu_custom_call" | custom-call | tf_op jit(solution)/shard_map/pallas_call | solution.py:331
  29.2 0.0 copy-start
  29.2 1.5 %copy-done = bf16[7200,128]{1,0:T(8,128)(2,1)S(1)} copy-done((bf16[7200,128]{1,0:T(8,128)(2,1)S(1)}, bf16[7200,128]{1,0:T(8,128)(2,1)}, u32[]{:S(2)}) %copy-start) | copy-done | bytes 1843224
  30.7 1.2 %shard_map.56 = bf16[7200,128]{1,0:T(8,128)(2,1)} custom-call(bf16[7200,128]{1,0:T(8,128)(2,1)S(1)} %copy-done), custom_call_target="tpu_custom_call" | custom-call | tf_op jit(solution)/shard_map/pallas_call | solution.py:364
Async XLA Ops:
  29.2 1.5 %copy-start = (bf16[7200,128]{1,0:T(8,128)(2,1)S(1)}, bf16[7200,128]{1,0:T(8,128)(2,1)}, u32[]{:S(2)}) copy-start(bf16[7200,128]{1,0:T(8,128)(2,1)} %shard_map.55.held) | copy-start | bytes 5529604
where the time goes:
time: 32.1 us; the launch traced here: 31.9 us
  Pallas kernels  29.1 us (91%)
  local copies, waits for them, and re-layouts  2.79 us (9%)
    pallas_call x1, Pallas kernels, shards(): pl.pallas_call(functools.partial(kernel, rows_x, chunks, plus_runs, minus...  27.9 us
    unnamed x2, local copies, waits for them, and re-layouts  1.5 us
    reshape x1, local copies, waits for them, and re-layouts, shards(): speeds.reshape(1, comps)  1.3 us
    pallas_call x1, Pallas kernels, shards(): pl.pallas_call(flush, out_shape=jax.ShapeDtypeStruct((comps * rows_x, lan...  1.24 us

commit v1 on v0

v1 whole, which is shorter than its diff:
```python
import functools
import math

import jax
import jax.numpy as jnp
import numpy as np
from jax import lax
from jax.experimental import pallas as pl
from jax.experimental.pallas import tpu as pltpu
from jax.sharding import PartitionSpec as P

ND = 36
PROP = 2
SUB = 16
UNIT = 72
PIECES = 9

coupling = 0.5


def circle():
    angle = np.arange(ND, dtype=np.int32).astype(np.float32) * np.float32(2.0 * math.pi / ND)
    angle = angle.astype(np.float64)
    return np.cos(angle).astype(np.float32), np.sin(angle).astype(np.float32)


def classes():
    cosine, sine = circle()
    key = [(bool(c > 0), bool(s >= 0)) for c, s in zip(cosine, sine)]
    first = next(d for d in range(ND) if key[d][0] and not key[d - 1][0])
    found = []
    for i in range(ND):
        d = (first + i) % ND
        if found and d > 0 and found[-1][0] == key[d]:
            found[-1][1].append(d)
        else:
            found.append((key[d], [d]))
    assert [k[0] for k, _ in found] == sorted((k[0] for k, _ in found), reverse=True)
    return found


def plan(comps):
    freqs = comps // ND
    groups, rest = freqs // SUB, freqs % SUB
    chunks = []
    for g in range(groups):
        main = [
            (g * SUB * ND + d, ND, SUB, up_x, up_y) for (up_x, up_y), run in classes() for d in run
        ]
        tail = []
        if g == groups - 1:
            tail = [
                ((groups * SUB + f) * ND + run[0], 1, len(run), up_x, up_y)
                for f in range(rest)
                for (up_x, up_y), run in classes()
            ]
            tail.sort(key=lambda t: t[0])
        tiles = [t for t in tail if t[3]] + main + [t for t in tail if not t[3]]
        ups = sum(t[3] for t in tiles)
        begin = g * SUB * ND
        end = comps if g == groups - 1 else begin + SUB * ND
        chunks.append((begin, end, tiles, ups))
    return chunks


def kernel(
    rows_x, chunks, counts,
    spec_hbm, inter_hbm, speeds_ref, mask_ref, stage,
    specv, inter, flat, acc, field, first, column, coefs, seas,
    xrecv, ysend, yrecv,
    load_sem, send_sem, recv_sem,
):
    comps, width = flat.shape
    lanes = width // rows_x
    f32, bf16 = jnp.float32, jnp.bfloat16
    px, sy = lax.axis_index("pts"), lax.axis_index("sub")
    nx, ny = counts
    partner = [{"pts": px + 1}, {"pts": px - 1}, {"sub": sy + 1}, {"sub": sy - 1}]
    sends = [px < nx - 1, px > 0, sy < ny - 1, sy > 0]
    receives = [sends[1], sends[0], sends[3], sends[2]]
    total = len(chunks)
    bases = list(np.cumsum([0] + [len(tiles) for _, _, tiles, _ in chunks]))

    spec_copy = pltpu.make_async_copy(spec_hbm, specv, load_sem.at[total])
    spec_copy.start()
    inter_copies = []
    for c, (begin, end, _, _) in enumerate(chunks):
        part = pl.ds(begin, end - begin)
        copy = pltpu.make_async_copy(inter_hbm.at[part], inter.at[part], load_sem.at[c])
        copy.start()
        inter_copies.append(copy)

    barrier = pltpu.get_barrier_semaphore()
    for kind in range(4):
        @pl.when(sends[kind])
        def _():
            pl.semaphore_signal(
                barrier, inc=1, device_id=partner[kind], device_id_type=pl.DeviceIdType.MESH
            )

    def exchange(e, c, kind):
        _, _, tiles, ups = chunks[c]
        if kind < 2:
            begin, count = (bases[c], ups) if kind == 0 else (bases[c] + ups, len(tiles) - ups)
            part = pl.ds(begin, count)
            source = (field if e == 0 else first).at[rows_x - 1 if kind == 0 else 0, part]
            target = xrecv.at[e, part]
        else:
            source, target = ysend.at[e, c], yrecv.at[e, kind - 2, c]
        return pltpu.make_async_remote_copy(
            src_ref=source, dst_ref=target,
            send_sem=send_sem.at[e, c, kind], recv_sem=recv_sem.at[e, c, kind],
            device_id=partner[kind], device_id_type=pl.DeviceIdType.MESH,
        )

    def start_sends(e, c):
        for kind in range(4):
            @pl.when(sends[kind])
            def _():
                exchange(e, c, kind).start()

    def wait_receives(e, c):
        for kind in range(4):
            @pl.when(receives[kind])
            def _():
                exchange(e, c, kind).wait_recv()

    for kind in range(2):
        @pl.when(jnp.logical_not(receives[kind]))
        def _():
            for e in range(PROP):
                for c, (_, _, tiles, ups) in enumerate(chunks):
                    begin, end = (0, ups) if kind == 0 else (ups, len(tiles))

                    @pl.loop(bases[c] + begin, bases[c] + end)
                    def _(t):
                        xrecv[e, t] = jnp.zeros(xrecv.shape[2:], bf16)

        @pl.when(jnp.logical_not(receives[kind + 2]))
        def _():
            for e in range(PROP):
                yrecv[e, kind] = jnp.zeros(yrecv.shape[2:], bf16)

    def lane_of(i, up_y):
        return 2 * i if up_y else 2 * i + 1

    starts = list(range(0, comps - lanes + 1, lanes))
    for at in starts:
        row = jnp.broadcast_to(speeds_ref[at : at + lanes].reshape(1, lanes), (lanes, lanes))
        column[at : at + lanes, :] = row.T
    done = starts[-1] + lanes
    if done < comps:
        row = jnp.broadcast_to(speeds_ref[done:comps].reshape(1, comps - done), (lanes, comps - done))
        column[done:comps, :] = row.T
    extra = column.shape[0] - comps
    column[comps : comps + extra, :] = jnp.zeros((extra, lanes), f32)
    stage[comps * rows_x : (comps + extra) * rows_x, :] = jnp.zeros((extra * rows_x, lanes), f32)

    cosine, sine = (np.abs(v) for v in circle())
    row_id = lax.broadcasted_iota(jnp.int32, (SUB, lanes), 0)
    for c, (_, _, tiles, _) in enumerate(chunks):
        for i, (k0, stride, real, _, _) in enumerate(tiles):
            speed = column[pl.ds(k0, SUB, stride=stride), :]
            if stride == 1:
                cx = jnp.zeros((SUB, lanes), f32)
                sx = jnp.zeros((SUB, lanes), f32)
                for r in range(real):
                    here = row_id == r
                    cx = jnp.where(here, float(cosine[(k0 + r) % ND]), cx)
                    sx = jnp.where(here, float(sine[(k0 + r) % ND]), sx)
                cross, along = speed * cx, speed * sx
            else:
                cross, along = speed * float(cosine[k0 % ND]), speed * float(sine[k0 % ND])
            coefs[bases[c] + i, 0] = 1.0 - cross - along
            coefs[bases[c] + i, 1] = cross
            coefs[bases[c] + i, 2] = along

    lane = lax.broadcasted_iota(jnp.int32, (SUB, lanes), 1)
    lane_f = lane.astype(f32).astype(bf16)
    parity = (lane % 2).astype(f32).astype(bf16)
    seaf = [
        jnp.broadcast_to(mask_ref[x : x + 1, :].astype(f32), (SUB, lanes)).astype(bf16)
        for x in range(rows_x)
    ]
    for i in range(seas.shape[0]):
        for x in range(rows_x):
            seas[i, x] = pltpu.roll(seaf[x], 2 * i + 1, 1)

    spec_copy.wait()

    small = mask_ref[...].astype(f32) * coupling
    sea_natural = jnp.concatenate([small] * (8 // rows_x), axis=0)

    def spread(block, count):
        length = count * UNIT
        begin = pl.multiple_of(block * (rows_x * UNIT), 16)
        whole = specv[pl.ds(begin, rows_x * length), :].astype(f32)
        whole = (whole.reshape(-1, 8, lanes) * sea_natural[None]).reshape(rows_x * length, lanes)
        stage[pl.ds(begin, rows_x * length), :] = whole
        for x in range(rows_x):
            values = stage[pl.ds(begin + x, length, stride=rows_x), :]
            flat[pl.ds(pl.multiple_of(block * UNIT, 8), length), x * lanes : (x + 1) * lanes] = (
                values.astype(bf16)
            )

    blocks = comps // UNIT

    @pl.loop(0, blocks // 2)
    def _(i):
        spread(2 * i, 2)

    if blocks % 2:
        spread(blocks - 1, 1)

    pl.semaphore_wait(barrier, sum(s.astype(jnp.int32) for s in sends))

    def grow(c):
        begin, end, tiles, _ = chunks[c]
        inter_copies[c].wait()
        product = jnp.dot(inter[begin:end, :], flat[...], preferred_element_type=f32)
        for x in range(rows_x):
            acc[x, 0 : end - begin, :] = product[:, x * lanes : (x + 1) * lanes]
        message = [jnp.zeros((SUB, lanes), bf16)] * rows_x
        for i, (k0, stride, _, _, up_y) in enumerate(tiles):
            mine = lane_f == float(lane_of(i, up_y))
            for x in range(rows_x):
                coupled = acc[x, pl.ds(k0 - begin, SUB, stride=stride), :]
                wide = stage[pl.ds(k0 * rows_x + x, SUB, stride=stride * rows_x), :]
                grown = (wide + wide * coupled).astype(bf16)
                grown = pltpu.roll(grown, 2 * i + 1, 1)
                field[x, bases[c] + i] = grown
                message[x] = jnp.where(mine, grown, message[x])
        for x in range(rows_x):
            ysend[0, c, x] = message[x]
        start_sends(0, c)

    def advance(e, c):
        _, _, tiles, _ = chunks[c]
        wait_receives(e, c)
        source = field if e == 0 else first
        even = parity == 0.0
        edges = [
            jnp.where(even, yrecv[e, 0, c, x], yrecv[e, 1, c, x]) for x in range(rows_x)
        ]
        message = [jnp.zeros((SUB, lanes), bf16)] * rows_x
        order = sorted(range(len(tiles)), key=lambda i: (tiles[i][1] == 1, tiles[i][0]))
        for i in order:
            k0, stride, _, up_x, up_y = tiles[i]
            t = bases[c] + i
            mine = lane_f == float(lane_of(i, up_y))
            keep, cross, along = (coefs[t, n].astype(bf16) for n in range(3))
            rows = [source[x, t] for x in range(rows_x)]
            outer = xrecv[e, t]
            for x in range(rows_x):
                if up_x:
                    near_x = rows[x - 1] if x > 0 else outer
                else:
                    near_x = rows[x + 1] if x < rows_x - 1 else outer
                near_y = pltpu.roll(
                    jnp.where(mine, edges[x], rows[x]), 1 if up_y else lanes - 1, 1
                )
                result = keep * rows[x] + cross * near_x + along * near_y
                if e == 0:
                    result = result * seas[i, x]
                    first[x, t] = result
                    message[x] = jnp.where(mine, result, message[x])
                else:
                    result = pltpu.roll(result, lanes - (2 * i + 1), 1)
                    stage[pl.ds(k0 * rows_x + x, SUB, stride=stride * rows_x), :] = (
                        result.astype(f32)
                    )
        if e == 0:
            for x in range(rows_x):
                ysend[1, c, x] = message[x]
            start_sends(1, c)

    for c in range(total):
        grow(c)
        if c >= 1:
            advance(0, c - 1)
    advance(0, total - 1)
    for c in range(total):
        advance(1, c)

    for e in range(PROP):
        for c in range(total):
            for kind in range(4):
                @pl.when(sends[kind])
                def _():
                    exchange(e, c, kind).wait_send()


def flush(rows_x, stage, mask_ref, out_hbm, outv, sem):
    lanes = outv.shape[1]
    piece = outv.shape[0] // PIECES
    twice = mask_ref[...].astype(jnp.float32) * (1.0 / coupling)
    sea = jnp.concatenate([twice] * (8 // rows_x), axis=0)
    copies = []
    for n in range(PIECES):
        part = pl.ds(n * piece, piece)
        values = stage[part, :].reshape(-1, 8, lanes) * sea[None]
        outv[part, :] = values.reshape(piece, lanes).astype(outv.dtype)
        copy = pltpu.make_async_copy(outv.at[part], out_hbm.at[part], sem.at[n])
        copy.start()
        copies.append(copy)
    for copy in copies:
        copy.wait()


def shards(mesh_counts, spectrum, interaction, speeds, mask):
    comps, rows_x, lanes = spectrum.shape
    chunks = plan(comps)
    total = len(chunks)
    tiles = sum(len(t) for _, _, t, _ in chunks)
    most = max(len(t) for _, _, t, _ in chunks)
    longest = max(end - begin for begin, end, _, _ in chunks)
    any_space = pl.BlockSpec(memory_space=pltpu.HBM)
    vmem = pl.BlockSpec(memory_space=pltpu.VMEM)
    f32, bf16 = jnp.float32, jnp.bfloat16
    stage = pl.pallas_call(
        functools.partial(kernel, rows_x, chunks, mesh_counts),
        out_shape=jax.ShapeDtypeStruct(((comps + SUB) * rows_x, lanes), f32),
        in_specs=[any_space, any_space, vmem, vmem],
        out_specs=vmem,
        scratch_shapes=[
            pltpu.VMEM((comps * rows_x, lanes), bf16),
            pltpu.VMEM((comps, comps), bf16),
            pltpu.VMEM((comps, rows_x * lanes), bf16),
            pltpu.VMEM((rows_x, longest + SUB, lanes), f32),
            pltpu.VMEM((rows_x, tiles, SUB, lanes), bf16),
            pltpu.VMEM((rows_x, tiles, SUB, lanes), bf16),
            pltpu.VMEM((comps + SUB, lanes), f32),
            pltpu.VMEM((tiles, 3, SUB, lanes), f32),
            pltpu.VMEM((most, rows_x, SUB, lanes), bf16),
            pltpu.VMEM((PROP, tiles, SUB, lanes), bf16),
            pltpu.VMEM((PROP, total, rows_x, SUB, lanes), bf16),
            pltpu.VMEM((PROP, 2, total, rows_x, SUB, lanes), bf16),
            pltpu.SemaphoreType.DMA((total + 1,)),
            pltpu.SemaphoreType.DMA((PROP, total, 4)),
            pltpu.SemaphoreType.DMA((PROP, total, 4)),
        ],
        compiler_params=pltpu.CompilerParams(
            collective_id=0, has_side_effects=True, vmem_limit_bytes=40 * 1024 * 1024
        ),
    )(spectrum.reshape(comps * rows_x, lanes), interaction, speeds, mask)
    out = pl.pallas_call(
        functools.partial(flush, rows_x),
        out_shape=jax.ShapeDtypeStruct((comps * rows_x, lanes), bf16),
        in_specs=[vmem, vmem],
        out_specs=any_space,
        scratch_shapes=[
            pltpu.VMEM((comps * rows_x, lanes), bf16),
            pltpu.SemaphoreType.DMA((PIECES,)),
        ],
        compiler_params=pltpu.CompilerParams(vmem_limit_bytes=12 * 1024 * 1024),
    )(stage, mask)
    return out.reshape(comps, rows_x, lanes)


def solution(mesh):
    placed = (P(None, ("member", "pts"), "sub"), P(), P(), P("pts", "sub"))
    return jax.shard_map(
        functools.partial(shards, (mesh.shape["pts"], mesh.shape["sub"])),
        mesh=mesh,
        in_specs=placed,
        out_specs=P(None, ("member", "pts"), "sub"),
        check_vma=False,
    )
```

time: 32.1 us -> 27.6 us (0.86)
  Pallas kernels: 29.1 us -> 21.5 us
  local copies, waits for them, and re-layouts: 2.79 us -> 5.84 us
    pallas_call x2, Pallas kernels: 29.1 us -> 21.5 us  [the longest x1 20.2 us: shards(): pl.pallas_call(functools.partial(kernel, rows_x, chunks, mesh_counts), ou...]
    unnamed x2 -> x8, local copies, waits for them, and re-layouts: 1.5 us -> 5.84 us
    reshape x1 -> x0, local copies, waits for them, and re-layouts: 1.3 us -> none  [shards(): speeds.reshape(1, comps)]
where the time goes in v1:
time: 27.6 us; the launch traced here: 27.3 us
  Pallas kernels  21.5 us (78%)
  local copies, waits for them, and re-layouts  5.84 us (21%)
    pallas_call x1, Pallas kernels, shards(): pl.pallas_call(functools.partial(kernel, rows_x, chunks, mesh_counts), ou...  20.2 us
    unnamed x8, local copies, waits for them, and re-layouts  5.84 us
    pallas_call x1, Pallas kernels, shards(): pl.pallas_call(functools.partial(flush, rows_x), out_shape=jax.ShapeDtype...  1.33 us

profile of v1, /device:TPU:0, one launch (start us, length us, event | category | flops | bytes accessed | tf_op | source)
XLA Modules:
  0.0 27.3 jit_solution(8440443675238100002)
XLA Ops:
  0.0 0.0 copy-start
  0.0 3.0 %copy-done = bf16[1800,1800]{1,0:T(8,128)(2,1)S(1)} copy-done((bf16[1800,1800]{1,0:T(8,128)(2,1)S(1)}, bf16[1800,1800]{1,0:T(8,128)(2,1)}, u32[]{:S(2)}) %copy-start) | copy-done | bytes 6480024
  3.0 0.0 copy-start.1
  3.0 1.5 %copy-done.1 = bf16[1800,4,128]{2,1,0:T(4,128)(2,1)S(1)} copy-done((bf16[1800,4,128]{2,1,0:T(4,128)(2,1)S(1)}, bf16[1800,4,128]{2,1,0:T(4,128)(2,1)}, u32[]{:S(2)}) %copy-start.1) | copy-done | bytes 1843224
  4.5 0.0 copy-start.2
  4.5 0.7 %copy-done.2 = s32[4,128]{1,0:T(4,128)S(1)} copy-done((s32[4,128]{1,0:T(4,128)S(1)}, s32[4,128]{1,0:T(4,128)}, u32[]{:S(2)}) %copy-start.2) | copy-done | bytes 2072
  5.1 0.0 copy-start.3
  5.1 0.7 %copy-done.3 = f32[1800]{0:T(1024)S(1)} copy-done((f32[1800]{0:T(1024)S(1)}, f32[1800]{0:T(1024)}, u32[]{:S(2)}) %copy-start.3) | copy-done | bytes 7224
  5.8 20.2 %shard_map.46.stage = f32[7264,128]{1,0:T(8,128)S(1)} custom-call(bf16[7200,128]{1,0:T(8,128)(2,1)S(1)} %bitcast.2, bf16[1800,1800]{1,0:T(8,128)(2,1)S(1)} %copy-done, f32[1800]{0:T(1024)S(1)} %copy-done.3, s32[4,128]{1,0:T(4,128)S(1)} %copy-done.2), custom_call_target="tpu_custom_call" | custom-call | tf_op jit(solution)/shard_map/pallas_call | solution.py:320
  26.0 1.3 %shard_map.47 = bf16[7200,128]{1,0:T(8,128)(2,1)} custom-call(f32[7264,128]{1,0:T(8,128)S(1)} %shard_map.46.stage, s32[4,128]{1,0:T(4,128)S(1)} %copy-done.2), custom_call_target="tpu_custom_call" | custom-call | tf_op jit(solution)/shard_map/pallas_call | solution.py:346
Async XLA Ops:
  0.0 3.0 %copy-start = (bf16[1800,1800]{1,0:T(8,128)(2,1)S(1)}, bf16[1800,1800]{1,0:T(8,128)(2,1)}, u32[]{:S(2)}) copy-start(bf16[1800,1800]{1,0:T(8,128)(2,1)} %inter_hbm.1) | copy-start | bytes 19440004
  3.0 1.5 %copy-start.1 = (bf16[1800,4,128]{2,1,0:T(4,128)(2,1)S(1)}, bf16[1800,4,128]{2,1,0:T(4,128)(2,1)}, u32[]{:S(2)}) copy-start(bf16[1800,4,128]{2,1,0:T(4,128)(2,1)} %param.4) | copy-start | bytes 5529604
  4.5 0.7 %copy-start.2 = (s32[4,128]{1,0:T(4,128)S(1)}, s32[4,128]{1,0:T(4,128)}, u32[]{:S(2)}) copy-start(s32[4,128]{1,0:T(4,128)} %mask_ref.3) | copy-start | bytes 6148
  5.1 0.7 %copy-start.3 = (f32[1800]{0:T(1024)S(1)}, f32[1800]{0:T(1024)}, u32[]{:S(2)}) copy-start(f32[1800]{0:T(1024)} %speeds_ref.1) | copy-start | bytes 21604

commit v2 on v1

--- a/solution.py
+++ b/solution.py
@@ -12,8 +12,8 @@
 ND = 36
 PROP = 2
 SUB = 16
-UNIT = 72
-PIECES = 9
+PIECES = 10
+PAD = 4
 
 coupling = 0.5
 
@@ -63,10 +63,15 @@
     return chunks
 
 
+def pitch(rows_x):
+    step = ND * rows_x + PAD
+    return step if step % 8 else step + PAD
+
+
 def kernel(
     rows_x, chunks, counts,
-    spec_hbm, inter_hbm, speeds_ref, mask_ref, stage,
-    specv, inter, flat, acc, field, first, column, coefs, seas,
+    spec_hbm, inter_hbm, speeds_hbm, mask_hbm, stage,
+    speeds_ref, mask_ref, specv, inter, flat, acc, field, first, column, coefs, seas,
     xrecv, ysend, yrecv,
     load_sem, send_sem, recv_sem,
 ):
@@ -79,8 +84,13 @@
     sends = [px < nx - 1, px > 0, sy < ny - 1, sy > 0]
     receives = [sends[1], sends[0], sends[3], sends[2]]
     total = len(chunks)
+    step = pitch(rows_x)
     bases = list(np.cumsum([0] + [len(tiles) for _, _, tiles, _ in chunks]))
 
+    speeds_copy = pltpu.make_async_copy(speeds_hbm, speeds_ref, load_sem.at[total + 1])
+    speeds_copy.start()
+    mask_copy = pltpu.make_async_copy(mask_hbm, mask_ref, load_sem.at[total + 2])
+    mask_copy.start()
     spec_copy = pltpu.make_async_copy(spec_hbm, specv, load_sem.at[total])
     spec_copy.start()
     inter_copies = []
@@ -144,6 +154,9 @@
     def lane_of(i, up_y):
         return 2 * i if up_y else 2 * i + 1
 
+    speeds_copy.wait()
+    mask_copy.wait()
+
     starts = list(range(0, comps - lanes + 1, lanes))
     for at in starts:
         row = jnp.broadcast_to(speeds_ref[at : at + lanes].reshape(1, lanes), (lanes, lanes))
@@ -154,7 +167,11 @@
         column[done:comps, :] = row.T
     extra = column.shape[0] - comps
     column[comps : comps + extra, :] = jnp.zeros((extra, lanes), f32)
-    stage[comps * rows_x : (comps + extra) * rows_x, :] = jnp.zeros((extra * rows_x, lanes), f32)
+    used = comps // ND * step
+    stage[used:, :] = jnp.zeros((stage.shape[0] - used, lanes), f32)
+    stage[stage.shape[0] - 8 :, :] = jnp.concatenate(
+        [mask_ref[...].astype(f32) * (1.0 / coupling)] * (8 // rows_x), axis=0
+    )
 
     cosine, sine = (np.abs(v) for v in circle())
     row_id = lax.broadcasted_iota(jnp.int32, (SUB, lanes), 0)
@@ -191,28 +208,32 @@
     small = mask_ref[...].astype(f32) * coupling
     sea_natural = jnp.concatenate([small] * (8 // rows_x), axis=0)
 
-    def spread(block, count):
-        length = count * UNIT
-        begin = pl.multiple_of(block * (rows_x * UNIT), 16)
-        whole = specv[pl.ds(begin, rows_x * length), :].astype(f32)
-        whole = (whole.reshape(-1, 8, lanes) * sea_natural[None]).reshape(rows_x * length, lanes)
-        stage[pl.ds(begin, rows_x * length), :] = whole
+    low = lax.broadcasted_iota(jnp.int32, (8, lanes), 0) < ND % 8
+    whole_rows = ND // 8 * 8
+
+    @pl.loop(0, comps // (2 * ND))
+    def _(block):
+        length = ND * rows_x
+        begin = pl.multiple_of(block * (2 * length), 16)
+        home = pl.multiple_of(block * (2 * step), 8)
+        values = specv[pl.ds(begin, 2 * length), :].astype(f32)
+        values = (values.reshape(-1, 8, lanes) * sea_natural[None]).reshape(2 * length, lanes)
+        stage[pl.ds(home, length), :] = values[:length]
+        stage[pl.ds(home + step, length), :] = values[length:]
         for x in range(rows_x):
-            values = stage[pl.ds(begin + x, length, stride=rows_x), :]
-            flat[pl.ds(pl.multiple_of(block * UNIT, 8), length), x * lanes : (x + 1) * lanes] = (
-                values.astype(bf16)
+            one = stage[pl.ds(home + x, whole_rows + 8, stride=rows_x), :]
+            two = stage[pl.ds(home + step - ND % 8 * rows_x + x, whole_rows + 8, stride=rows_x), :]
+            middle = jnp.where(low, one[whole_rows:], two[:8])
+            both = jnp.concatenate([one[:whole_rows], middle, two[8:]], axis=0)
+            flat[pl.ds(pl.multiple_of(block * (2 * ND), 8), 2 * ND), x * lanes : (x + 1) * lanes] = (
+                both.astype(bf16)
             )
 
-    blocks = comps // UNIT
-
-    @pl.loop(0, blocks // 2)
-    def _(i):
-        spread(2 * i, 2)
-
-    if blocks % 2:
-        spread(blocks - 1, 1)
-
     pl.semaphore_wait(barrier, sum(s.astype(jnp.int32) for s in sends))
+
+    def staged(k0, stride, x):
+        begin = k0 // ND * step + k0 % ND * rows_x + x
+        return pl.ds(begin, SUB, stride=rows_x if stride == 1 else step)
 
     def grow(c):
         begin, end, tiles, _ = chunks[c]
@@ -225,7 +246,7 @@
             mine = lane_f == float(lane_of(i, up_y))
             for x in range(rows_x):
                 coupled = acc[x, pl.ds(k0 - begin, SUB, stride=stride), :]
-                wide = stage[pl.ds(k0 * rows_x + x, SUB, stride=stride * rows_x), :]
+                wide = stage[staged(k0, stride, x), :]
                 grown = (wide + wide * coupled).astype(bf16)
                 grown = pltpu.roll(grown, 2 * i + 1, 1)
                 field[x, bases[c] + i] = grown
@@ -266,9 +287,7 @@
                     message[x] = jnp.where(mine, result, message[x])
                 else:
                     result = pltpu.roll(result, lanes - (2 * i + 1), 1)
-                    stage[pl.ds(k0 * rows_x + x, SUB, stride=stride * rows_x), :] = (
-                        result.astype(f32)
-                    )
+                    stage[staged(k0, stride, x), :] = result.astype(f32)
         if e == 0:
             for x in range(rows_x):
                 ysend[1, c, x] = message[x]
@@ -290,16 +309,19 @@
                     exchange(e, c, kind).wait_send()
 
 
-def flush(rows_x, stage, mask_ref, out_hbm, outv, sem):
+def flush(rows_x, stage, out_hbm, outv, sem):
     lanes = outv.shape[1]
-    piece = outv.shape[0] // PIECES
-    twice = mask_ref[...].astype(jnp.float32) * (1.0 / coupling)
-    sea = jnp.concatenate([twice] * (8 // rows_x), axis=0)
+    length, step = ND * rows_x, pitch(rows_x)
+    freqs = outv.shape[0] // length
+    pieces = sem.shape[0]
+    each = freqs // pieces
+    sea = stage[stage.shape[0] - 8 :, :]
     copies = []
-    for n in range(PIECES):
-        part = pl.ds(n * piece, piece)
-        values = stage[part, :].reshape(-1, 8, lanes) * sea[None]
-        outv[part, :] = values.reshape(piece, lanes).astype(outv.dtype)
+    for n in range(pieces):
+        for f in range(n * each, (n + 1) * each):
+            values = stage[f * step : f * step + length, :].reshape(-1, 8, lanes) * sea[None]
+            outv[f * length : (f + 1) * length, :] = values.reshape(length, lanes).astype(outv.dtype)
+        part = pl.ds(n * each * length, each * length)
         copy = pltpu.make_async_copy(outv.at[part], out_hbm.at[part], sem.at[n])
         copy.start()
         copies.append(copy)
@@ -317,12 +339,19 @@
     any_space = pl.BlockSpec(memory_space=pltpu.HBM)
     vmem = pl.BlockSpec(memory_space=pltpu.VMEM)
     f32, bf16 = jnp.float32, jnp.bfloat16
+    freqs = comps // ND
+    pieces = next(n for n in range(PIECES, 0, -1) if freqs % n == 0)
+    held = -(-(freqs * pitch(rows_x) + SUB * rows_x) // 8) * 8 + 8
+    grant = 40 * 1024 * 1024
+    pin = functools.partial(pltpu.with_memory_space_constraint, memory_space=pltpu.HBM)
     stage = pl.pallas_call(
         functools.partial(kernel, rows_x, chunks, mesh_counts),
-        out_shape=jax.ShapeDtypeStruct(((comps + SUB) * rows_x, lanes), f32),
-        in_specs=[any_space, any_space, vmem, vmem],
+        out_shape=jax.ShapeDtypeStruct((held, lanes), f32),
+        in_specs=[any_space] * 4,
         out_specs=vmem,
         scratch_shapes=[
+            pltpu.VMEM(speeds.shape, f32),
+            pltpu.VMEM(mask.shape, mask.dtype),
             pltpu.VMEM((comps * rows_x, lanes), bf16),
             pltpu.VMEM((comps, comps), bf16),
             pltpu.VMEM((comps, rows_x * lanes), bf16),
@@ -335,25 +364,25 @@
             pltpu.VMEM((PROP, tiles, SUB, lanes), bf16),
             pltpu.VMEM((PROP, total, rows_x, SUB, lanes), bf16),
             pltpu.VMEM((PROP, 2, total, rows_x, SUB, lanes), bf16),
-            pltpu.SemaphoreType.DMA((total + 1,)),
+            pltpu.SemaphoreType.DMA((total + 3,)),
             pltpu.SemaphoreType.DMA((PROP, total, 4)),
             pltpu.SemaphoreType.DMA((PROP, total, 4)),
         ],
         compiler_params=pltpu.CompilerParams(
-            collective_id=0, has_side_effects=True, vmem_limit_bytes=40 * 1024 * 1024
+            collective_id=0, has_side_effects=True, vmem_limit_bytes=grant
         ),
-    )(spectrum.reshape(comps * rows_x, lanes), interaction, speeds, mask)
+    )(pin(spectrum.reshape(comps * rows_x, lanes)), pin(interaction), pin(speeds), pin(mask))
     out = pl.pallas_call(
         functools.partial(flush, rows_x),
         out_shape=jax.ShapeDtypeStruct((comps * rows_x, lanes), bf16),
-        in_specs=[vmem, vmem],
+        in_specs=[vmem],
         out_specs=any_space,
         scratch_shapes=[
             pltpu.VMEM((comps * rows_x, lanes), bf16),
-            pltpu.SemaphoreType.DMA((PIECES,)),
+            pltpu.SemaphoreType.DMA((pieces,)),
         ],
         compiler_params=pltpu.CompilerParams(vmem_limit_bytes=12 * 1024 * 1024),
-    )(stage, mask)
+    )(stage)
     return out.reshape(comps, rows_x, lanes)
 
 

time: 27.6 us -> 20.5 us (0.74)
  local copies, waits for them, and re-layouts: 5.84 us -> 0 us
  Pallas kernels: 21.5 us -> 20.3 us
    unnamed x8 -> x0, local copies, waits for them, and re-layouts: 5.84 us -> none
    pallas_call x1, Pallas kernels: 20.2 us -> 18.9 us  [shards(): pl.pallas_call(functools.partial(kernel, rows_x, chunks, mesh_counts), ou...]
where the time goes in v2:
time: 20.5 us; the launch traced here: 20.3 us
  Pallas kernels  20.3 us (99%)
    pallas_call x1, Pallas kernels, shards(): pl.pallas_call(functools.partial(kernel, rows_x, chunks, mesh_counts), ou...  18.9 us
    pallas_call x1, Pallas kernels, shards(): pl.pallas_call(functools.partial(flush, rows_x), out_shape=jax.ShapeDtype...  1.33 us

profile of v2, /device:TPU:0, one launch (start us, length us, event | category | flops | bytes accessed | tf_op | source)
XLA Modules:
  0.0 20.3 jit_solution(6230703193195572669)
XLA Ops:
  0.0 18.9 %shard_map.46.stage = f32[7472,128]{1,0:T(8,128)S(1)} custom-call(bf16[7200,128]{1,0:T(8,128)(2,1)} %bitcast.2, bf16[1800,1800]{1,0:T(8,128)(2,1)} %inter_hbm.1, f32[1800]{0:T(1024)} %speeds_hbm.1, s32[4,128]{1,0:T(4,128)} %mask_hbm.1), custom_call_target="tpu_custom_call" | custom-call | tf_op jit(solution)/shard_map/pallas_call | solution.py:347
  19.0 1.3 %shard_map.47 = bf16[7200,128]{1,0:T(8,128)(2,1)} custom-call(f32[7472,128]{1,0:T(8,128)S(1)} %shard_map.46.stage), custom_call_target="tpu_custom_call" | custom-call | tf_op jit(solution)/shard_map/pallas_call | solution.py:375

commit v3 on v2

--- a/solution.py
+++ b/solution.py
@@ -12,6 +12,10 @@
 ND = 36
 PROP = 2
 SUB = 16
+HALF = 8
+SIZES = (1, 2, 2, 1)
+LAG = 3
+LOADS = 5
 PIECES = 10
 PAD = 4
 
@@ -41,25 +45,36 @@
 
 def plan(comps):
     freqs = comps // ND
-    groups, rest = freqs // SUB, freqs % SUB
-    chunks = []
-    for g in range(groups):
-        main = [
-            (g * SUB * ND + d, ND, SUB, up_x, up_y) for (up_x, up_y), run in classes() for d in run
-        ]
-        tail = []
-        if g == groups - 1:
-            tail = [
-                ((groups * SUB + f) * ND + run[0], 1, len(run), up_x, up_y)
-                for f in range(rest)
-                for (up_x, up_y), run in classes()
-            ]
-            tail.sort(key=lambda t: t[0])
-        tiles = [t for t in tail if t[3]] + main + [t for t in tail if not t[3]]
-        ups = sum(t[3] for t in tiles)
-        begin = g * SUB * ND
-        end = comps if g == groups - 1 else begin + SUB * ND
-        chunks.append((begin, end, tiles, ups))
+    groups, rest = freqs // HALF, freqs % HALF
+    sizes, left = [], groups
+    for size in SIZES:
+        size = min(size, left)
+        if size:
+            sizes.append(size)
+            left -= size
+    while left:
+        sizes.insert(1, min(2, left))
+        left -= sizes[1]
+    chunks, top = [], groups
+    for n, size in enumerate(sizes):
+        tiles = []
+        for g in range(top - size, top):
+            for (up_x, up_y), run in classes():
+                for pair in [run[i : i + 2] for i in range(0, len(run), 2)]:
+                    pair = (pair * 2)[:2]
+                    tiles.append(([(g * HALF * ND + d, ND, [d] * HALF) for d in pair], up_x, up_y))
+        begin, end = (top - size) * HALF * ND, top * HALF * ND
+        if n == 0:
+            end = comps
+            for f in range(rest):
+                for (up_x, up_y), run in sorted(classes(), key=lambda c: c[1][0]):
+                    ds = run + [None] * (SUB - len(run))
+                    k0 = (groups * HALF + f) * ND + run[0]
+                    parts = [(k0, 1, ds[:HALF]), (k0 + HALF, 1, ds[HALF:])]
+                    tiles.append((parts, up_x, up_y))
+        tiles.sort(key=lambda t: not t[1])
+        chunks.append((begin, end, tiles, sum(t[1] for t in tiles)))
+        top -= size
     return chunks
 
 
@@ -87,12 +102,20 @@
     step = pitch(rows_x)
     bases = list(np.cumsum([0] + [len(tiles) for _, _, tiles, _ in chunks]))
 
-    speeds_copy = pltpu.make_async_copy(speeds_hbm, speeds_ref, load_sem.at[total + 1])
+    speeds_copy = pltpu.make_async_copy(speeds_hbm, speeds_ref, load_sem.at[total])
     speeds_copy.start()
-    mask_copy = pltpu.make_async_copy(mask_hbm, mask_ref, load_sem.at[total + 2])
+    mask_copy = pltpu.make_async_copy(mask_hbm, mask_ref, load_sem.at[total + 1])
     mask_copy.start()
-    spec_copy = pltpu.make_async_copy(spec_hbm, specv, load_sem.at[total])
-    spec_copy.start()
+    blocks = comps // (2 * ND)
+    loads = next(n for n in range(LOADS, 0, -1) if blocks % n == 0)
+    piece = comps * rows_x // loads
+
+    def spec_copy(n):
+        part = pl.ds(pl.multiple_of(n * piece, 16), piece)
+        return pltpu.make_async_copy(spec_hbm.at[part], specv.at[part], load_sem.at[total + 2 + n])
+
+    for n in range(loads):
+        spec_copy(n).start()
     inter_copies = []
     for c, (begin, end, _, _) in enumerate(chunks):
         part = pl.ds(begin, end - begin)
@@ -174,23 +197,26 @@
     )
 
     cosine, sine = (np.abs(v) for v in circle())
-    row_id = lax.broadcasted_iota(jnp.int32, (SUB, lanes), 0)
+    row_id = lax.broadcasted_iota(jnp.int32, (HALF, lanes), 0)
+
+    def factor(values, directions):
+        found = [float(values[d]) if d is not None else 0.0 for d in directions]
+        if len(set(found)) == 1:
+            return found[0]
+        column = jnp.zeros((HALF, lanes), f32)
+        for r, value in enumerate(found):
+            column = jnp.where(row_id == r, value, column)
+        return column
+
     for c, (_, _, tiles, _) in enumerate(chunks):
-        for i, (k0, stride, real, _, _) in enumerate(tiles):
-            speed = column[pl.ds(k0, SUB, stride=stride), :]
-            if stride == 1:
-                cx = jnp.zeros((SUB, lanes), f32)
-                sx = jnp.zeros((SUB, lanes), f32)
-                for r in range(real):
-                    here = row_id == r
-                    cx = jnp.where(here, float(cosine[(k0 + r) % ND]), cx)
-                    sx = jnp.where(here, float(sine[(k0 + r) % ND]), sx)
-                cross, along = speed * cx, speed * sx
-            else:
-                cross, along = speed * float(cosine[k0 % ND]), speed * float(sine[k0 % ND])
-            coefs[bases[c] + i, 0] = 1.0 - cross - along
-            coefs[bases[c] + i, 1] = cross
-            coefs[bases[c] + i, 2] = along
+        for i, (parts, _, _) in enumerate(tiles):
+            for h, (k0, stride, directions) in enumerate(parts):
+                rows = slice(h * HALF, (h + 1) * HALF)
+                speed = column[pl.ds(k0, HALF, stride=stride), :]
+                cross, along = speed * factor(cosine, directions), speed * factor(sine, directions)
+                coefs[bases[c] + i, 0, rows] = 1.0 - cross - along
+                coefs[bases[c] + i, 1, rows] = cross
+                coefs[bases[c] + i, 2, rows] = along
 
     lane = lax.broadcasted_iota(jnp.int32, (SUB, lanes), 1)
     lane_f = lane.astype(f32).astype(bf16)
@@ -203,16 +229,13 @@
         for x in range(rows_x):
             seas[i, x] = pltpu.roll(seaf[x], 2 * i + 1, 1)
 
-    spec_copy.wait()
-
     small = mask_ref[...].astype(f32) * coupling
     sea_natural = jnp.concatenate([small] * (8 // rows_x), axis=0)
 
     low = lax.broadcasted_iota(jnp.int32, (8, lanes), 0) < ND % 8
     whole_rows = ND // 8 * 8
 
-    @pl.loop(0, comps // (2 * ND))
-    def _(block):
+    def spread(block):
         length = ND * rows_x
         begin = pl.multiple_of(block * (2 * length), 16)
         home = pl.multiple_of(block * (2 * step), 8)
@@ -229,11 +252,18 @@
                 both.astype(bf16)
             )
 
+    @pl.loop(0, loads)
+    def _(n):
+        spec_copy(n).wait()
+        for i in range(blocks // loads):
+            spread(n * (blocks // loads) + i)
+
     pl.semaphore_wait(barrier, sum(s.astype(jnp.int32) for s in sends))
 
-    def staged(k0, stride, x):
+    def staged(part, x):
+        k0, stride, _ = part
         begin = k0 // ND * step + k0 % ND * rows_x + x
-        return pl.ds(begin, SUB, stride=rows_x if stride == 1 else step)
+        return pl.ds(begin, HALF, stride=rows_x if stride == 1 else step)
 
     def grow(c):
         begin, end, tiles, _ = chunks[c]
@@ -242,12 +272,16 @@
         for x in range(rows_x):
             acc[x, 0 : end - begin, :] = product[:, x * lanes : (x + 1) * lanes]
         message = [jnp.zeros((SUB, lanes), bf16)] * rows_x
-        for i, (k0, stride, _, _, up_y) in enumerate(tiles):
+        for i, (parts, _, up_y) in enumerate(tiles):
             mine = lane_f == float(lane_of(i, up_y))
             for x in range(rows_x):
-                coupled = acc[x, pl.ds(k0 - begin, SUB, stride=stride), :]
-                wide = stage[staged(k0, stride, x), :]
-                grown = (wide + wide * coupled).astype(bf16)
+                halves = []
+                for part in parts:
+                    k0, stride, _ = part
+                    coupled = acc[x, pl.ds(k0 - begin, HALF, stride=stride), :]
+                    wide = stage[staged(part, x), :]
+                    halves.append(wide + wide * coupled)
+                grown = jnp.concatenate(halves, axis=0).astype(bf16)
                 grown = pltpu.roll(grown, 2 * i + 1, 1)
                 field[x, bases[c] + i] = grown
                 message[x] = jnp.where(mine, grown, message[x])
@@ -264,9 +298,9 @@
             jnp.where(even, yrecv[e, 0, c, x], yrecv[e, 1, c, x]) for x in range(rows_x)
         ]
         message = [jnp.zeros((SUB, lanes), bf16)] * rows_x
-        order = sorted(range(len(tiles)), key=lambda i: (tiles[i][1] == 1, tiles[i][0]))
+        order = sorted(range(len(tiles)), key=lambda i: (tiles[i][0][0][1] == 1, tiles[i][0][0][0]))
         for i in order:
-            k0, stride, _, up_x, up_y = tiles[i]
+            parts, up_x, up_y = tiles[i]
             t = bases[c] + i
             mine = lane_f == float(lane_of(i, up_y))
             keep, cross, along = (coefs[t, n].astype(bf16) for n in range(3))
@@ -287,7 +321,9 @@
                     message[x] = jnp.where(mine, result, message[x])
                 else:
                     result = pltpu.roll(result, lanes - (2 * i + 1), 1)
-                    stage[staged(k0, stride, x), :] = result.astype(f32)
+                    result = result.astype(f32)
+                    for h, part in enumerate(parts):
+                        stage[staged(part, x), :] = result[h * HALF : (h + 1) * HALF]
         if e == 0:
             for x in range(rows_x):
                 ysend[1, c, x] = message[x]
@@ -295,9 +331,10 @@
 
     for c in range(total):
         grow(c)
-        if c >= 1:
-            advance(0, c - 1)
-    advance(0, total - 1)
+        if c >= LAG:
+            advance(0, c - LAG)
+    for c in range(max(total - LAG, 0), total):
+        advance(0, c)
     for c in range(total):
         advance(1, c)
 
@@ -364,7 +401,7 @@
             pltpu.VMEM((PROP, tiles, SUB, lanes), bf16),
             pltpu.VMEM((PROP, total, rows_x, SUB, lanes), bf16),
             pltpu.VMEM((PROP, 2, total, rows_x, SUB, lanes), bf16),
-            pltpu.SemaphoreType.DMA((total + 3,)),
+            pltpu.SemaphoreType.DMA((total + 2 + LOADS,)),
             pltpu.SemaphoreType.DMA((PROP, total, 4)),
             pltpu.SemaphoreType.DMA((PROP, total, 4)),
         ],

time: 20.5 us -> 18 us (0.88)
  Pallas kernels: 20.3 us -> 17.8 us
    pallas_call x1, Pallas kernels: 18.9 us -> 16.4 us  [shards(): pl.pallas_call(functools.partial(kernel, rows_x, chunks, mesh_counts), ou...]
where the time goes in v3:
time: 18 us; the launch traced here: 17.8 us
  Pallas kernels  17.8 us (99%)
    pallas_call x1, Pallas kernels, shards(): pl.pallas_call(functools.partial(kernel, rows_x, chunks, mesh_counts), ou...  16.4 us
    pallas_call x1, Pallas kernels, shards(): pl.pallas_call(functools.partial(flush, rows_x), out_shape=jax.ShapeDtype...  1.33 us

profile of v3, /device:TPU:0, one launch (start us, length us, event | category | flops | bytes accessed | tf_op | source)
XLA Modules:
  0.0 17.8 jit_solution(3258754004512507940)
XLA Ops:
  0.0 16.4 %shard_map.46.stage = f32[7472,128]{1,0:T(8,128)S(1)} custom-call(bf16[7200,128]{1,0:T(8,128)(2,1)} %bitcast.2, bf16[1800,1800]{1,0:T(8,128)(2,1)} %inter_hbm.1, f32[1800]{0:T(1024)} %speeds_hbm.1, s32[4,128]{1,0:T(4,128)} %mask_hbm.1), custom_call_target="tpu_custom_call" | custom-call | tf_op jit(solution)/shard_map/pallas_call | solution.py:384
  16.5 1.3 %shard_map.47 = bf16[7200,128]{1,0:T(8,128)(2,1)} custom-call(f32[7472,128]{1,0:T(8,128)S(1)} %shard_map.46.stage), custom_call_target="tpu_custom_call" | custom-call | tf_op jit(solution)/shard_map/pallas_call | solution.py:412

commit v4 on v3

--- a/solution.py
+++ b/solution.py
@@ -14,7 +14,6 @@
 SUB = 16
 HALF = 8
 SIZES = (1, 2, 2, 1)
-LAG = 3
 LOADS = 5
 PIECES = 10
 PAD = 4
@@ -87,17 +86,22 @@
     rows_x, chunks, counts,
     spec_hbm, inter_hbm, speeds_hbm, mask_hbm, stage,
     speeds_ref, mask_ref, specv, inter, flat, acc, field, first, column, coefs, seas,
-    xrecv, ysend, yrecv,
-    load_sem, send_sem, recv_sem,
+    packed, early, xrecv, ysend, yrecv, corner, own_sea, other_sea,
+    load_sem, send_sem, recv_sem, sea_send, sea_recv,
 ):
     comps, width = flat.shape
     lanes = width // rows_x
     f32, bf16 = jnp.float32, jnp.bfloat16
     px, sy = lax.axis_index("pts"), lax.axis_index("sub")
     nx, ny = counts
+    xs, ys = {1: px < nx - 1, -1: px > 0}, {1: sy < ny - 1, -1: sy > 0}
     partner = [{"pts": px + 1}, {"pts": px - 1}, {"sub": sy + 1}, {"sub": sy - 1}]
-    sends = [px < nx - 1, px > 0, sy < ny - 1, sy > 0]
-    receives = [sends[1], sends[0], sends[3], sends[2]]
+    sends, receives = [xs[1], xs[-1], ys[1], ys[-1]], [xs[-1], xs[1], ys[-1], ys[1]]
+    for dx in (1, -1):
+        for dy in (1, -1):
+            partner.append({"pts": px + dx, "sub": sy + dy})
+            sends.append(jnp.logical_and(xs[dx], ys[dy]))
+            receives.append(jnp.logical_and(xs[-dx], ys[-dy]))
     total = len(chunks)
     step = pitch(rows_x)
     bases = list(np.cumsum([0] + [len(tiles) for _, _, tiles, _ in chunks]))
@@ -124,55 +128,73 @@
         inter_copies.append(copy)
 
     barrier = pltpu.get_barrier_semaphore()
-    for kind in range(4):
+    for kind in range(8):
         @pl.when(sends[kind])
         def _():
             pl.semaphore_signal(
                 barrier, inc=1, device_id=partner[kind], device_id_type=pl.DeviceIdType.MESH
             )
 
-    def exchange(e, c, kind):
+    def exchange(c, slot):
         _, _, tiles, ups = chunks[c]
-        if kind < 2:
+        if slot < 4:
+            kind = slot % 2
             begin, count = (bases[c], ups) if kind == 0 else (bases[c] + ups, len(tiles) - ups)
             part = pl.ds(begin, count)
-            source = (field if e == 0 else first).at[rows_x - 1 if kind == 0 else 0, part]
-            target = xrecv.at[e, part]
+            source = field.at[rows_x - 1 if kind == 0 else 0, part] if slot < 2 else early.at[part]
+            target = xrecv.at[slot // 2, part]
+        elif slot < 6:
+            kind = slot - 2
+            source, target = ysend.at[c], yrecv.at[kind - 2, c]
         else:
-            source, target = ysend.at[e, c], yrecv.at[e, kind - 2, c]
-        return pltpu.make_async_remote_copy(
+            kind = slot - 2
+            source, target = ysend.at[c, 0, rows_x - 1 if kind < 6 else 0], corner.at[kind - 4, c]
+        return kind, pltpu.make_async_remote_copy(
             src_ref=source, dst_ref=target,
-            send_sem=send_sem.at[e, c, kind], recv_sem=recv_sem.at[e, c, kind],
+            send_sem=send_sem.at[c, slot], recv_sem=recv_sem.at[c, slot],
             device_id=partner[kind], device_id_type=pl.DeviceIdType.MESH,
         )
 
-    def start_sends(e, c):
-        for kind in range(4):
+    def send_sea(kind):
+        return pltpu.make_async_remote_copy(
+            src_ref=own_sea, dst_ref=other_sea.at[kind],
+            send_sem=sea_send.at[kind], recv_sem=sea_recv.at[kind],
+            device_id=partner[kind], device_id_type=pl.DeviceIdType.MESH,
+        )
+
+    def start_sends(c):
+        for slot in (4, 5, 6, 7, 8, 9, 0, 1, 2, 3):
+            kind, copy = exchange(c, slot)
+
             @pl.when(sends[kind])
             def _():
-                exchange(e, c, kind).start()
-
-    def wait_receives(e, c):
-        for kind in range(4):
+                copy.start()
+
+    def wait_receives(c):
+        for slot in range(10):
+            kind, copy = exchange(c, slot)
+
             @pl.when(receives[kind])
             def _():
-                exchange(e, c, kind).wait_recv()
-
-    for kind in range(2):
+                copy.wait_recv()
+
+    for kind in range(8):
         @pl.when(jnp.logical_not(receives[kind]))
         def _():
-            for e in range(PROP):
+            if kind < 4:
+                other_sea[kind] = jnp.zeros(other_sea.shape[1:], bf16)
+            if kind < 2:
                 for c, (_, _, tiles, ups) in enumerate(chunks):
                     begin, end = (0, ups) if kind == 0 else (ups, len(tiles))
 
                     @pl.loop(bases[c] + begin, bases[c] + end)
                     def _(t):
-                        xrecv[e, t] = jnp.zeros(xrecv.shape[2:], bf16)
-
-        @pl.when(jnp.logical_not(receives[kind + 2]))
-        def _():
-            for e in range(PROP):
-                yrecv[e, kind] = jnp.zeros(yrecv.shape[2:], bf16)
+                        for e in range(2):
+                            xrecv[e, t] = jnp.zeros(xrecv.shape[2:], bf16)
+            elif kind < 4:
+                yrecv[kind - 2] = jnp.zeros(yrecv.shape[1:], bf16)
+            else:
+                corner[kind - 4] = jnp.zeros(corner.shape[1:], bf16)
 
     def lane_of(i, up_y):
         return 2 * i if up_y else 2 * i + 1
@@ -208,19 +230,28 @@
             column = jnp.where(row_id == r, value, column)
         return column
 
+    lane = lax.broadcasted_iota(jnp.int32, (SUB, lanes), 1)
+    lane_f = lane.astype(f32).astype(bf16)
+    even = (lane % 2).astype(f32).astype(bf16) == 0.0
+
     for c, (_, _, tiles, _) in enumerate(chunks):
-        for i, (parts, _, _) in enumerate(tiles):
+        together = [jnp.zeros((SUB, lanes), bf16)] * 3
+        for i, (parts, _, up_y) in enumerate(tiles):
+            mine = lane_f == float(lane_of(i, up_y))
+            weights = [[], [], []]
             for h, (k0, stride, directions) in enumerate(parts):
                 rows = slice(h * HALF, (h + 1) * HALF)
                 speed = column[pl.ds(k0, HALF, stride=stride), :]
                 cross, along = speed * factor(cosine, directions), speed * factor(sine, directions)
-                coefs[bases[c] + i, 0, rows] = 1.0 - cross - along
-                coefs[bases[c] + i, 1, rows] = cross
-                coefs[bases[c] + i, 2, rows] = along
-
-    lane = lax.broadcasted_iota(jnp.int32, (SUB, lanes), 1)
-    lane_f = lane.astype(f32).astype(bf16)
-    parity = (lane % 2).astype(f32).astype(bf16)
+                for n, value in enumerate((1.0 - cross - along, cross, along)):
+                    coefs[bases[c] + i, n, rows] = value
+                    weights[n].append(value)
+            for n in range(3):
+                value = jnp.concatenate(weights[n], axis=0).astype(bf16)
+                together[n] = jnp.where(mine, value, together[n])
+        for n in range(3):
+            packed[c, n] = together[n]
+
     seaf = [
         jnp.broadcast_to(mask_ref[x : x + 1, :].astype(f32), (SUB, lanes)).astype(bf16)
         for x in range(rows_x)
@@ -229,7 +260,24 @@
         for x in range(rows_x):
             seas[i, x] = pltpu.roll(seaf[x], 2 * i + 1, 1)
 
-    small = mask_ref[...].astype(f32) * coupling
+    rows_sea = mask_ref[...].astype(f32)
+    own_sea[...] = jnp.concatenate(
+        [rows_sea, jnp.zeros((SUB - rows_x, lanes), f32)], axis=0
+    ).astype(bf16)
+    line = lax.broadcasted_iota(jnp.int32, (1, lanes), 1)
+
+    def splat(row, at):
+        value = jnp.sum(jnp.where(line == at, row, 0.0), axis=1, keepdims=True)
+        return jnp.broadcast_to(value, (SUB, lanes)).astype(bf16)
+
+    edge_sea = [
+        jnp.where(even, splat(rows_sea[x : x + 1], lanes - 1), splat(rows_sea[x : x + 1], 0))
+        for x in range(rows_x)
+    ]
+    for x in range(rows_x):
+        packed[total, x] = edge_sea[x]
+
+    small = rows_sea * coupling
     sea_natural = jnp.concatenate([small] * (8 // rows_x), axis=0)
 
     low = lax.broadcasted_iota(jnp.int32, (8, lanes), 0) < ND % 8
@@ -259,53 +307,75 @@
             spread(n * (blocks // loads) + i)
 
     pl.semaphore_wait(barrier, sum(s.astype(jnp.int32) for s in sends))
+    for kind in range(4):
+        @pl.when(sends[kind])
+        def _():
+            send_sea(kind).start()
 
     def staged(part, x):
         k0, stride, _ = part
         begin = k0 // ND * step + k0 % ND * rows_x + x
         return pl.ds(begin, HALF, stride=rows_x if stride == 1 else step)
 
-    def grow(c):
-        begin, end, tiles, _ = chunks[c]
+    def multiply(c):
+        begin, end, _, _ = chunks[c]
         inter_copies[c].wait()
         product = jnp.dot(inter[begin:end, :], flat[...], preferred_element_type=f32)
         for x in range(rows_x):
-            acc[x, 0 : end - begin, :] = product[:, x * lanes : (x + 1) * lanes]
-        message = [jnp.zeros((SUB, lanes), bf16)] * rows_x
-        for i, (parts, _, up_y) in enumerate(tiles):
+            acc[c % 2, x, 0 : end - begin, :] = product[:, x * lanes : (x + 1) * lanes]
+
+    def below(c):
+        return lane_f < float(2 * chunks[c][3])
+
+    def grow(c):
+        begin, end, tiles, _ = chunks[c]
+        none = jnp.zeros((SUB, lanes), bf16)
+        message, second = [none] * rows_x, [none] * rows_x
+        for i, (parts, up_x, up_y) in enumerate(tiles):
+            t = bases[c] + i
             mine = lane_f == float(lane_of(i, up_y))
+            next_lane = lane_f == float((lane_of(i, up_y) + (lanes - 1 if up_y else 1)) % lanes)
+            rows = []
             for x in range(rows_x):
                 halves = []
                 for part in parts:
                     k0, stride, _ = part
-                    coupled = acc[x, pl.ds(k0 - begin, HALF, stride=stride), :]
+                    coupled = acc[c % 2, x, pl.ds(k0 - begin, HALF, stride=stride), :]
                     wide = stage[staged(part, x), :]
                     halves.append(wide + wide * coupled)
                 grown = jnp.concatenate(halves, axis=0).astype(bf16)
                 grown = pltpu.roll(grown, 2 * i + 1, 1)
-                field[x, bases[c] + i] = grown
+                rows.append(grown)
+                field[x, t] = grown
                 message[x] = jnp.where(mine, grown, message[x])
+                second[x] = jnp.where(next_lane, grown, second[x])
+            keep, cross, along = (coefs[t, n].astype(bf16) for n in range(3))
+            edge, inner = (rows_x - 1, rows_x - 2) if up_x else (0, 1)
+            near_y = pltpu.roll(jnp.where(mine, none, rows[edge]), 1 if up_y else lanes - 1, 1)
+            result = keep * rows[edge] + cross * rows[inner] + along * near_y
+            early[t] = result * seas[i, edge]
         for x in range(rows_x):
-            ysend[0, c, x] = message[x]
-        start_sends(0, c)
-
-    def advance(e, c):
+            near_y = jnp.where(even, pltpu.roll(second[x], 1, 1), pltpu.roll(second[x], lanes - 1, 1))
+            near_x = jnp.where(
+                below(c),
+                message[x - 1] if x > 0 else none,
+                message[x + 1] if x < rows_x - 1 else none,
+            )
+            result = packed[c, 0] * message[x] + packed[c, 1] * near_x + packed[c, 2] * near_y
+            ysend[c, 0, x] = message[x]
+            ysend[c, 1, x] = result * packed[total, x]
+        start_sends(c)
+
+    def step_one(c):
         _, _, tiles, _ = chunks[c]
-        wait_receives(e, c)
-        source = field if e == 0 else first
-        even = parity == 0.0
-        edges = [
-            jnp.where(even, yrecv[e, 0, c, x], yrecv[e, 1, c, x]) for x in range(rows_x)
-        ]
-        message = [jnp.zeros((SUB, lanes), bf16)] * rows_x
-        order = sorted(range(len(tiles)), key=lambda i: (tiles[i][0][0][1] == 1, tiles[i][0][0][0]))
-        for i in order:
-            parts, up_x, up_y = tiles[i]
+        wait_receives(c)
+        edges = [jnp.where(even, yrecv[0, c, 0, x], yrecv[1, c, 0, x]) for x in range(rows_x)]
+        for i, (_, up_x, up_y) in enumerate(tiles):
             t = bases[c] + i
             mine = lane_f == float(lane_of(i, up_y))
             keep, cross, along = (coefs[t, n].astype(bf16) for n in range(3))
-            rows = [source[x, t] for x in range(rows_x)]
-            outer = xrecv[e, t]
+            rows = [field[x, t] for x in range(rows_x)]
+            outer = xrecv[0, t]
             for x in range(rows_x):
                 if up_x:
                     near_x = rows[x - 1] if x > 0 else outer
@@ -315,35 +385,93 @@
                     jnp.where(mine, edges[x], rows[x]), 1 if up_y else lanes - 1, 1
                 )
                 result = keep * rows[x] + cross * near_x + along * near_y
-                if e == 0:
-                    result = result * seas[i, x]
-                    first[x, t] = result
-                    message[x] = jnp.where(mine, result, message[x])
+                first[x, t] = result * seas[i, x]
+
+    def neighbours_sea():
+        for kind in range(4):
+            @pl.when(receives[kind])
+            def _():
+                send_sea(kind).wait_recv()
+        from_low, from_high, from_left, from_right = (
+            other_sea[kind].astype(f32) for kind in range(4)
+        )
+        last = rows_x - 1
+
+        def columns(x):
+            return jnp.where(
+                even, splat(from_left[x : x + 1], lanes - 1), splat(from_right[x : x + 1], 0)
+            )
+
+        packed[total + 1, 0] = columns(0)
+        packed[total + 1, 1] = columns(last)
+        packed[total + 1, 2] = splat(from_low[last : last + 1], 0)
+        packed[total + 1, 3] = splat(from_high[0:1], 0)
+        packed[total + 2, 0] = splat(from_low[last : last + 1], lanes - 1)
+        packed[total + 2, 1] = splat(from_high[0:1], lanes - 1)
+
+    def step_two(c):
+        _, _, tiles, _ = chunks[c]
+        low = below(c)
+        none = jnp.zeros((SUB, lanes), bf16)
+        corners = jnp.where(
+            low,
+            jnp.where(even, corner[0, c], corner[1, c]),
+            jnp.where(even, corner[2, c], corner[3, c]),
+        )
+        edges = [jnp.where(even, yrecv[0, c, 1, x], yrecv[1, c, 1, x]) for x in range(rows_x)]
+        missing = corners * packed[c, 1]
+        last = rows_x - 1
+        edges[0] = edges[0] + jnp.where(low, missing * packed[total + 1, 0], none)
+        edges[last] = edges[last] + jnp.where(low, none, missing * packed[total + 1, 1])
+        turned = {
+            True: pltpu.roll(corners, 1, 1)
+            * jnp.where(low, packed[total + 1, 2], packed[total + 1, 3]),
+            False: pltpu.roll(corners, lanes - 1, 1)
+            * jnp.where(low, packed[total + 2, 0], packed[total + 2, 1]),
+        }
+        order = sorted(range(len(tiles)), key=lambda i: (tiles[i][0][0][1] == 1, tiles[i][0][0][0]))
+        for i in order:
+            parts, up_x, up_y = tiles[i]
+            t = bases[c] + i
+            mine = lane_f == float(lane_of(i, up_y))
+            there = lane_f == float(lane_of(i, not up_y))
+            keep, cross, along = (coefs[t, n].astype(bf16) for n in range(3))
+            rows = [first[x, t] for x in range(rows_x)]
+            outer = jnp.where(there, along * turned[up_y], none) + xrecv[1, t]
+            for x in range(rows_x):
+                if up_x:
+                    near_x = rows[x - 1] if x > 0 else outer
                 else:
-                    result = pltpu.roll(result, lanes - (2 * i + 1), 1)
-                    result = result.astype(f32)
-                    for h, part in enumerate(parts):
-                        stage[staged(part, x), :] = result[h * HALF : (h + 1) * HALF]
-        if e == 0:
-            for x in range(rows_x):
-                ysend[1, c, x] = message[x]
-            start_sends(1, c)
-
+                    near_x = rows[x + 1] if x < last else outer
+                near_y = pltpu.roll(
+                    jnp.where(mine, edges[x], rows[x]), 1 if up_y else lanes - 1, 1
+                )
+                result = keep * rows[x] + cross * near_x + along * near_y
+                result = pltpu.roll(result, lanes - (2 * i + 1), 1).astype(f32)
+                for h, part in enumerate(parts):
+                    stage[staged(part, x), :] = result[h * HALF : (h + 1) * HALF]
+
+    multiply(0)
+    for c in range(1, total):
+        multiply(c)
+        grow(c - 1)
+    grow(total - 1)
+    neighbours_sea()
     for c in range(total):
-        grow(c)
-        if c >= LAG:
-            advance(0, c - LAG)
-    for c in range(max(total - LAG, 0), total):
-        advance(0, c)
+        step_one(c)
+        step_two(c)
+
+    for kind in range(4):
+        @pl.when(sends[kind])
+        def _():
+            send_sea(kind).wait_send()
     for c in range(total):
-        advance(1, c)
-
-    for e in range(PROP):
-        for c in range(total):
-            for kind in range(4):
-                @pl.when(sends[kind])
-                def _():
-                    exchange(e, c, kind).wait_send()
+        for slot in range(10):
+            kind, copy = exchange(c, slot)
+
+            @pl.when(sends[kind])
+            def _():
+                copy.wait_send()
 
 
 def flush(rows_x, stage, out_hbm, outv, sem):
@@ -392,18 +520,25 @@
             pltpu.VMEM((comps * rows_x, lanes), bf16),
             pltpu.VMEM((comps, comps), bf16),
             pltpu.VMEM((comps, rows_x * lanes), bf16),
-            pltpu.VMEM((rows_x, longest + SUB, lanes), f32),
+            pltpu.VMEM((2, rows_x, longest + SUB, lanes), f32),
             pltpu.VMEM((rows_x, tiles, SUB, lanes), bf16),
             pltpu.VMEM((rows_x, tiles, SUB, lanes), bf16),
             pltpu.VMEM((comps + SUB, lanes), f32),
             pltpu.VMEM((tiles, 3, SUB, lanes), f32),
             pltpu.VMEM((most, rows_x, SUB, lanes), bf16),
+            pltpu.VMEM((total + 3, max(rows_x, 4), SUB, lanes), bf16),
+            pltpu.VMEM((tiles, SUB, lanes), bf16),
             pltpu.VMEM((PROP, tiles, SUB, lanes), bf16),
-            pltpu.VMEM((PROP, total, rows_x, SUB, lanes), bf16),
-            pltpu.VMEM((PROP, 2, total, rows_x, SUB, lanes), bf16),
+            pltpu.VMEM((total, PROP, rows_x, SUB, lanes), bf16),
+            pltpu.VMEM((2, total, PROP, rows_x, SUB, lanes), bf16),
+            pltpu.VMEM((4, total, SUB, lanes), bf16),
+            pltpu.VMEM((SUB, lanes), bf16),
+            pltpu.VMEM((4, SUB, lanes), bf16),
             pltpu.SemaphoreType.DMA((total + 2 + LOADS,)),
-            pltpu.SemaphoreType.DMA((PROP, total, 4)),
-            pltpu.SemaphoreType.DMA((PROP, total, 4)),
+            pltpu.SemaphoreType.DMA((total, 10)),
+            pltpu.SemaphoreType.DMA((total, 10)),
+            pltpu.SemaphoreType.DMA((4,)),
+            pltpu.SemaphoreType.DMA((4,)),
         ],
         compiler_params=pltpu.CompilerParams(
             collective_id=0, has_side_effects=True, vmem_limit_bytes=grant

time: 18 us -> 16.8 us (0.933)
  the two profiles are of different devices: /device:TPU:0 before, /device:TPU:1 now
where the time goes in v4:
time: 16.8 us; the launch traced here: 16.6 us
  Pallas kernels  16.6 us (99%)
    pallas_call x1, Pallas kernels, shards(): pl.pallas_call(functools.partial(kernel, rows_x, chunks, mesh_counts), ou...  15.2 us
    pallas_call x1, Pallas kernels, shards(): pl.pallas_call(functools.partial(flush, rows_x), out_shape=jax.ShapeDtype...  1.33 us

profile of v4, /device:TPU:1, one launch (start us, length us, event | category | flops | bytes accessed | tf_op | source)
XLA Modules:
  0.0 16.6 jit_solution(5820509659627549852)
XLA Ops:
  0.0 15.2 %shard_map.46.stage = f32[7472,128]{1,0:T(8,128)S(1)} custom-call(bf16[7200,128]{1,0:T(8,128)(2,1)} %bitcast.2, bf16[1800,1800]{1,0:T(8,128)(2,1)} %inter_hbm.1, f32[1800]{0:T(1024)} %speeds_hbm.1, s32[4,128]{1,0:T(4,128)} %mask_hbm.1), custom_call_target="tpu_custom_call" | custom-call | tf_op jit(solution)/shard_map/pallas_call | solution.py:512
  15.2 1.3 %shard_map.47 = bf16[7200,128]{1,0:T(8,128)(2,1)} custom-call(f32[7472,128]{1,0:T(8,128)S(1)} %shard_map.46.stage), custom_call_target="tpu_custom_call" | custom-call | tf_op jit(solution)/shard_map/pallas_call | solution.py:547

commit v5 on v4

--- a/solution.py
+++ b/solution.py
@@ -52,18 +52,26 @@
             sizes.append(size)
             left -= size
     while left:
-        sizes.insert(1, min(2, left))
-        left -= sizes[1]
-    chunks, top = [], groups
+        sizes.append(min(2, left))
+        left -= sizes[-1]
+    chunks, low = [], 0
     for n, size in enumerate(sizes):
         tiles = []
-        for g in range(top - size, top):
-            for (up_x, up_y), run in classes():
-                for pair in [run[i : i + 2] for i in range(0, len(run), 2)]:
-                    pair = (pair * 2)[:2]
-                    tiles.append(([(g * HALF * ND + d, ND, [d] * HALF) for d in pair], up_x, up_y))
-        begin, end = (top - size) * HALF * ND, top * HALF * ND
-        if n == 0:
+        first = low * HALF * ND
+        for (up_x, up_y), run in classes():
+            if size == 2:
+                pairs = [[first + d, first + HALF * ND + d] for d in run]
+            else:
+                pairs = [
+                    ([first + g * HALF * ND + d for d in run[i : i + 2]] * 2)[:2]
+                    for g in range(size)
+                    for i in range(0, len(run), 2)
+                ]
+            for pair in pairs:
+                tiles.append(([(k0, ND, [k0 % ND] * HALF) for k0 in pair], up_x, up_y))
+        low += size
+        end = low * HALF * ND
+        if n == len(sizes) - 1:
             end = comps
             for f in range(rest):
                 for (up_x, up_y), run in sorted(classes(), key=lambda c: c[1][0]):
@@ -72,8 +80,7 @@
                     parts = [(k0, 1, ds[:HALF]), (k0 + HALF, 1, ds[HALF:])]
                     tiles.append((parts, up_x, up_y))
         tiles.sort(key=lambda t: not t[1])
-        chunks.append((begin, end, tiles, sum(t[1] for t in tiles)))
-        top -= size
+        chunks.append((first, end, tiles, sum(t[1] for t in tiles)))
     return chunks
 
 
@@ -306,11 +313,12 @@
         for i in range(blocks // loads):
             spread(n * (blocks // loads) + i)
 
-    pl.semaphore_wait(barrier, sum(s.astype(jnp.int32) for s in sends))
-    for kind in range(4):
-        @pl.when(sends[kind])
-        def _():
-            send_sea(kind).start()
+    def enter():
+        pl.semaphore_wait(barrier, sum(s.astype(jnp.int32) for s in sends))
+        for kind in range(4):
+            @pl.when(sends[kind])
+            def _():
+                send_sea(kind).start()
 
     def staged(part, x):
         k0, stride, _ = part
@@ -452,10 +460,11 @@
                     stage[staged(part, x), :] = result[h * HALF : (h + 1) * HALF]
 
     multiply(0)
+    enter()
+    grow(0)
     for c in range(1, total):
         multiply(c)
-        grow(c - 1)
-    grow(total - 1)
+        grow(c)
     neighbours_sea()
     for c in range(total):
         step_one(c)

time: 16.8 us -> 16.3 us (0.970)
  Pallas kernels: 16.6 us -> 16.1 us
    pallas_call x1, Pallas kernels: 15.2 us -> 14.8 us  [shards(): pl.pallas_call(functools.partial(kernel, rows_x, chunks, mesh_counts), ou...]
where the time goes in v5:
time: 16.3 us; the launch traced here: 16.1 us
  Pallas kernels  16.1 us (99%)
    pallas_call x1, Pallas kernels, shards(): pl.pallas_call(functools.partial(kernel, rows_x, chunks, mesh_counts), ou...  14.8 us
    pallas_call x1, Pallas kernels, shards(): pl.pallas_call(functools.partial(flush, rows_x), out_shape=jax.ShapeDtype...  1.33 us

profile of v5, /device:TPU:1, one launch (start us, length us, event | category | flops | bytes accessed | tf_op | source)
XLA Modules:
  0.0 16.1 jit_solution(14305031514635802000)
XLA Ops:
  0.0 14.8 %shard_map.46.stage = f32[7472,128]{1,0:T(8,128)S(1)} custom-call(bf16[7200,128]{1,0:T(8,128)(2,1)} %bitcast.2, bf16[1800,1800]{1,0:T(8,128)(2,1)} %inter_hbm.1, f32[1800]{0:T(1024)} %speeds_hbm.1, s32[4,128]{1,0:T(4,128)} %mask_hbm.1), custom_call_target="tpu_custom_call" | custom-call | tf_op jit(solution)/shard_map/pallas_call | solution.py:521
  14.8 1.3 %shard_map.47 = bf16[7200,128]{1,0:T(8,128)(2,1)} custom-call(f32[7472,128]{1,0:T(8,128)S(1)} %shard_map.46.stage), custom_call_target="tpu_custom_call" | custom-call | tf_op jit(solution)/shard_map/pallas_call | solution.py:556
